TPU v7x, 32 devices: a whole 2x2x4 slice. The times are simulated.
32 devices in a mesh: seq: 32 (over z, y, x, core).
Axes of the slice: x: 2, y: 2, z: 4, core: 2. Of those that a mesh axis runs over, the one named last changes fastest.
Arguments:
- queries: bfloat16 [8192, 8, 128], P('seq'), may hold values from -132 to 132
- keys: bfloat16 [16384, 8, 128], P('seq'), may hold values from -6 to 6
- values: bfloat16 [16384, 8, 128], P('seq'), may hold values from -6 to 6
- routes: int32 [8192, 8], P('seq'), may hold values from 0 to 63, all different within a row; in each aligned block of 256 rows (0 to 255, 256 to 511, ...) at most 40 rows name the same one
Outputs:
- attended: bfloat16 [8192, 8, 128], P('seq')
Inputs may be any that keep to these rules, and one draw needn't show every extreme that they name: `routes`: each row names 8 different heads; among the 256 rows of one device no head is named more than 40 times, a bound that some block reaches.
All inputs are finite; a program needn't handle non-finite values.
Results may differ from a plain program's by a relative error of at most 0.0065.
Values may be sent and summed in bfloat16 or wider, within the bound.
A program may use at most 64 MiB of HBM per device.

v0:
```python
import jax
import jax.numpy as jnp
from jax import lax
from jax.sharding import PartitionSpec as P

HEADS = 64
HOPS = 4
MOST = 40


def shifted(block, axis, distance):
    devices = range(lax.axis_size(axis))
    route = [(i - distance, i) for i in devices if i - distance in devices]
    return lax.ppermute(block, axis, route)


def slot_index(routes):
    flat_heads = routes.reshape(-1)
    entries = flat_heads.shape[0]
    block_rows = 128
    block_count = entries // block_rows
    heads_all = jnp.arange(HEADS, dtype=jnp.int32)
    onehot = (flat_heads[:, None] == heads_all[None, :]).astype(jnp.bfloat16)
    blocks = onehot.reshape(block_count, block_rows, HEADS)
    inner = jnp.arange(block_rows, dtype=jnp.int32)
    lower = (inner[None, :] < inner[:, None]).astype(jnp.bfloat16)
    inside_block = jnp.einsum("ab,kbh->kah", lower, blocks, preferred_element_type=jnp.float32)
    block_totals = jnp.sum(blocks.astype(jnp.float32), axis=1).astype(jnp.bfloat16)
    outer = jnp.arange(block_count, dtype=jnp.int32)
    lower_blocks = (outer[None, :] < outer[:, None]).astype(jnp.bfloat16)
    block_start = jnp.dot(lower_blocks, block_totals, preferred_element_type=jnp.float32)
    before = (inside_block + block_start[:, None, :]).reshape(entries, HEADS)
    within = jnp.sum(before * onehot.astype(jnp.float32), axis=1).astype(jnp.int32)
    return flat_heads * MOST + within


def visit(state, packed, keys_shard, values_shard, allowed):
    running, highest, denominator = state
    width = packed.shape[2]
    scores = jnp.einsum("gqd,kgd->gqk", packed, keys_shard, preferred_element_type=jnp.float32)
    scores = scores / jnp.sqrt(jnp.float32(width))
    scores = jnp.where(allowed, scores, jnp.float32(-1e30))
    newest = jnp.maximum(highest, jnp.max(scores, axis=2))
    weights = jnp.where(allowed, jnp.exp(scores - newest[:, :, None]), jnp.float32(0.0))
    factor = jnp.exp(highest - newest)
    denominator = denominator * factor + jnp.sum(weights, axis=2)
    product = jnp.einsum(
        "gqk,kgd->gqd",
        weights.astype(jnp.bfloat16),
        values_shard,
        preferred_element_type=jnp.float32,
    )
    running = running * factor[:, :, None] + product
    return (running, newest, denominator)


def shards(queries, keys, values, routes):
    tokens_count, routed_count, width = queries.shape
    context_rows, groups, _ = keys.shape
    device = lax.axis_index("seq")
    slots = slot_index(routes)
    flat = queries.reshape(-1, width)
    slot_all = jnp.arange(HEADS * MOST, dtype=jnp.int32)
    placing = (slot_all[:, None] == slots[None, :]).astype(jnp.bfloat16)
    packed = jnp.dot(placing, flat, preferred_element_type=jnp.float32).astype(jnp.bfloat16)
    tokens_of = (jnp.arange(tokens_count * routed_count, dtype=jnp.int32) // routed_count).astype(
        jnp.float32
    )
    positions = jnp.dot(
        placing.astype(jnp.float32), tokens_of, precision=lax.Precision.HIGHEST
    ).astype(jnp.int32)
    packed = packed.reshape(groups, -1, width)
    positions = positions.reshape(groups, -1)
    rows_group = packed.shape[1]
    offset = context_rows - tokens_count
    own_mask = (
        jnp.arange(context_rows, dtype=jnp.int32)[None, None, :] <= (positions + offset)[:, :, None]
    )
    state = (
        jnp.zeros((groups, rows_group, width), jnp.float32),
        jnp.full((groups, rows_group), -1e30, jnp.float32),
        jnp.zeros((groups, rows_group), jnp.float32),
    )
    state = visit(state, packed, keys, values, own_mask)
    moving_keys, moving_values = (keys, values)
    for travel in range(1, HOPS + 1):
        moving_keys, moving_values = shifted((moving_keys, moving_values), "seq", 1)
        usable = device - travel >= 0
        state = visit(state, packed, moving_keys, moving_values, usable)
    finished = (state[0] / state[2][:, :, None]).astype(jnp.bfloat16)
    unpacked = jnp.einsum(
        "si,sd->id", placing, finished.reshape(-1, width), preferred_element_type=jnp.float32
    )
    return unpacked.astype(jnp.bfloat16).reshape(tokens_count, routed_count, width)


def solution(mesh):
    placed = (P("seq", None, None), P("seq", None, None), P("seq", None, None), P("seq", None))
    return jax.shard_map(
        shards, mesh=mesh, in_specs=placed, out_specs=P("seq", None, None), check_vma=False
    )
```

profile of v0, /device:TPU:16, one launch (start us, length us, event | category | flops | bytes accessed | tf_op | source)
XLA Modules:
  0.0 115.0 jit_solution(13047138744719753970)
XLA Ops:
  0.0 0.0 copy-start
  0.0 1.4 %copy.11 = bf16[512,8,128]{2,0,1:T(8,128)(2,1)S(1)} copy(bf16[512,8,128]{2,1,0:T(8,128)(2,1)} %param.5) | data formatting | bytes 2097152 | tf_op args[1]
  1.4 1.9 %collective-permute-start = (bf16[512,8,128]{2,0,1:T(8,128)(2,1)S(1)}, bf16[512,8,128]{2,0,1:T(8,128)(2,1)S(1)}, u32[]{:S(2)}, u32[]{:S(2)}) collective-permute-start(bf16[512,8,128]{2,0,1:T(8,128)(2,1)S(1)} %copy.11), channel_id=1, source_target_pairs={{0,1},{1,2},{2,3},{3,4},{4,5},{5,6},{6,7},{7,8},{8,9},{9,10},{10,1... | collective-permute-start | bytes 3145736 | tf_op jit(solution)/shard_map/ppermute | solution.py:14
  3.4 2.4 %copy.12 = bf16[512,8,128]{2,0,1:T(8,128)(2,1)} copy(bf16[512,8,128]{2,1,0:T(8,128)(2,1)} %param.6) | data formatting | bytes 2097152 | tf_op args[2]
  5.8 3.5 %collective-permute-start.1 = (bf16[512,8,128]{2,0,1:T(8,128)(2,1)}, bf16[512,8,128]{2,0,1:T(8,128)(2,1)}, u32[]{:S(2)}, u32[]{:S(2)}) collective-permute-start(bf16[512,8,128]{2,0,1:T(8,128)(2,1)} %copy.12), channel_id=1, source_target_pairs={{0,1},{1,2},{2,3},{3,4},{4,5},{5,6},{6,7},{7,8},{8,9},{9,10},{10,1... | collective-permute-start | bytes 3145736 | tf_op jit(solution)/shard_map/ppermute | solution.py:14
  9.3 10.1 %collective-permute-done = bf16[512,8,128]{2,0,1:T(8,128)(2,1)S(1)} collective-permute-done((bf16[512,8,128]{2,0,1:T(8,128)(2,1)S(1)}, bf16[512,8,128]{2,0,1:T(8,128)(2,1)S(1)}, u32[]{:S(2)}, u32[]{:S(2)}) %collective-permute-start) | collective-permute-done | bytes 1048608 | tf_op jit(solution)/shard_map/ppermute | solution.py:14
  19.3 1.9 %collective-permute-start.2 = (bf16[512,8,128]{2,0,1:T(8,128)(2,1)S(1)}, bf16[512,8,128]{2,0,1:T(8,128)(2,1)S(1)}, u32[]{:S(2)}, u32[]{:S(2)}) collective-permute-start(bf16[512,8,128]{2,0,1:T(8,128)(2,1)S(1)} %collective-permute-done), channel_id=1, source_target_pairs={{0,1},{1,2},{2,3},{3,4},{4,5},{5,6},{6,7},{7,8},{8,9},{9,10},{10,1... | collective-permute-start | bytes 3145736 | tf_op jit(solution)/shard_map/ppermute | solution.py:14
  21.3 0.8 copy.10
  22.1 0.1 eq.32
  22.2 0.7 broadcast_multiply_fusion
  22.9 0.1 copy.9
  23.0 0.1 mul.84
  23.2 0.2 fusion.73
  23.4 0.1 fusion.80
  23.5 0.3 fusion.67
  23.8 6.9 %collective-permute-done.1 = bf16[512,8,128]{2,0,1:T(8,128)(2,1)} collective-permute-done((bf16[512,8,128]{2,0,1:T(8,128)(2,1)}, bf16[512,8,128]{2,0,1:T(8,128)(2,1)}, u32[]{:S(2)}, u32[]{:S(2)}) %collective-permute-start.1) | collective-permute-done | bytes 1048608 | tf_op jit(solution)/shard_map/ppermute | solution.py:14
  30.7 1.9 %collective-permute-start.3 = (bf16[512,8,128]{2,0,1:T(8,128)(2,1)}, bf16[512,8,128]{2,0,1:T(8,128)(2,1)}, u32[]{:S(2)}, u32[]{:S(2)}) collective-permute-start(bf16[512,8,128]{2,0,1:T(8,128)(2,1)} %collective-permute-done.1), channel_id=1, source_target_pairs={{0,1},{1,2},{2,3},{3,4},{4,5},{5,6},{6,7},{7,8},{8,9},{9,10},{10,1... | collective-permute-start | bytes 3145736 | tf_op jit(solution)/shard_map/ppermute | solution.py:14
  32.6 9.2 %collective-permute-done.2 = bf16[512,8,128]{2,0,1:T(8,128)(2,1)S(1)} collective-permute-done((bf16[512,8,128]{2,0,1:T(8,128)(2,1)S(1)}, bf16[512,8,128]{2,0,1:T(8,128)(2,1)S(1)}, u32[]{:S(2)}, u32[]{:S(2)}) %collective-permute-start.2) | collective-permute-done | bytes 1048608 | tf_op jit(solution)/shard_map/ppermute | solution.py:14
  41.8 1.9 %collective-permute-start.4 = (bf16[512,8,128]{2,0,1:T(8,128)(2,1)S(1)}, bf16[512,8,128]{2,0,1:T(8,128)(2,1)}, u32[]{:S(2)}, u32[]{:S(2)}) collective-permute-start(bf16[512,8,128]{2,0,1:T(8,128)(2,1)S(1)} %collective-permute-done.2), channel_id=1, source_target_pairs={{0,1},{1,2},{2,3},{3,4},{4,5},{5,6},{6,7},{7,8},{8,9},{9,10},{10,1... | collective-permute-start | bytes 3145736 | tf_op jit(solution)/shard_map/ppermute | solution.py:14
  43.7 9.2 %fusion.68 = f32[2560]{0:T(1024)S(1)} fusion(f32[2048,1]{0,1:T(1,128)S(1)} %bitcast.40, s32[2048]{0:T(1024)S(1)} %bitcast_add_fusion), kind=kOutput, calls=%fused_computation.59 | convolution fusion | flops 68157440 | bytes 26624 | tf_op jit(solution)/shard_map/dot_general | solution.py:69
  53.0 0.1 add.92
  53.1 0.0 copy-done
  53.1 3.8 %fusion.19 = bf16[2560,128]{1,0:T(8,128)(2,1)S(1)} fusion(s32[2048]{0:T(1024)S(1)} %bitcast_add_fusion, bf16[256,8,128]{2,1,0:T(8,128)(2,1)S(1)} %copy-done), kind=kOutput, calls=%fused_computation.31 | convolution fusion | flops 1347747840 | bytes 1187840 | tf_op jit(solution)/shard_map/dot_general | solution.py:65
  56.9 0.0 collective-permute-done.3
  56.9 1.9 %collective-permute-start.5 = (bf16[512,8,128]{2,0,1:T(8,128)(2,1)}, bf16[512,8,128]{2,0,1:T(8,128)(2,1)S(1)}, u32[]{:S(2)}, u32[]{:S(2)}) collective-permute-start(bf16[512,8,128]{2,0,1:T(8,128)(2,1)} %collective-permute-done.3), channel_id=1, source_target_pairs={{0,1},{1,2},{2,3},{3,4},{4,5},{5,6},{6,7},{7,8},{8,9},{9,10},{10,1... | collective-permute-start | bytes 3145736 | tf_op jit(solution)/shard_map/ppermute | solution.py:14
  58.8 0.0 copy-done.1
  58.8 1.9 %fusion.10 = (f32[8,320]{1,0:T(8,128)S(1)}, f32[8,320,512]{2,1,0:T(8,128)S(1)}) fusion(s32[8,320]{1,0:T(8,128)S(1)} %add.92, bf16[8,320,128]{2,1,0:T(8,128)(2,1)S(1)} %bitcast.35, bf16[512,8,128]{2,1,0:T(8,128)(2,1)S(1)} %copy-done.1), kind=kOutput, calls=%fused_computation.22 | convolution fusion | flops 340784640 | bytes 6967296 | tf_op jit(solution)/shard_map/gqd,kgd->gqk/dot_general | solution.py:40
  60.7 3.7 %collective-permute-done.4 = bf16[512,8,128]{2,0,1:T(8,128)(2,1)} collective-permute-done((bf16[512,8,128]{2,0,1:T(8,128)(2,1)S(1)}, bf16[512,8,128]{2,0,1:T(8,128)(2,1)}, u32[]{:S(2)}, u32[]{:S(2)}) %collective-permute-start.4) | collective-permute-done | bytes 1048608 | tf_op jit(solution)/shard_map/ppermute | solution.py:14
  64.4 2.1 %collective-permute-start.6 = (bf16[512,8,128]{2,0,1:T(8,128)(2,1)}, bf16[512,8,128]{2,0,1:T(8,128)(2,1)S(1)}, u32[]{:S(2)}, u32[]{:S(2)}) collective-permute-start(bf16[512,8,128]{2,0,1:T(8,128)(2,1)} %collective-permute-done.4), channel_id=1, source_target_pairs={{0,1},{1,2},{2,3},{3,4},{4,5},{5,6},{6,7},{7,8},{8,9},{9,10},{10,1... | collective-permute-start | bytes 3145736 | tf_op jit(solution)/shard_map/ppermute | solution.py:14
  66.5 1.0 fusion.6
  67.4 1.0 fusion.7
  68.4 7.1 %collective-permute-done.5 = bf16[512,8,128]{2,0,1:T(8,128)(2,1)S(1)} collective-permute-done((bf16[512,8,128]{2,0,1:T(8,128)(2,1)}, bf16[512,8,128]{2,0,1:T(8,128)(2,1)S(1)}, u32[]{:S(2)}, u32[]{:S(2)}) %collective-permute-start.5) | collective-permute-done | bytes 1048608 | tf_op jit(solution)/shard_map/ppermute | solution.py:14
  75.5 1.9 %collective-permute-start.7 = (bf16[512,8,128]{2,0,1:T(8,128)(2,1)S(1)}, bf16[512,8,128]{2,0,1:T(8,128)(2,1)S(1)}, u32[]{:S(2)}, u32[]{:S(2)}) collective-permute-start(bf16[512,8,128]{2,0,1:T(8,128)(2,1)S(1)} %collective-permute-done.5), channel_id=1, source_target_pairs={{0,1},{1,2},{2,3},{3,4},{4,5},{5,6},{6,7},{7,8},{8,9},{9,10},{10,1... | collective-permute-start | bytes 3145736 | tf_op jit(solution)/shard_map/ppermute | solution.py:14
  77.4 2.2 %fusion.8 = (f32[8,320]{1,0:T(8,128)S(1)}, f32[8,320,512]{2,1,0:T(8,128)S(1)}) fusion(pred[]{:T(512)S(6)} %ge.14, bf16[8,320,128]{2,1,0:T(8,128)(2,1)S(1)} %bitcast.38, bf16[512,8,128]{2,0,1:T(8,128)(2,1)} %collective-permute-done.4), kind=kOutput, calls=%fused_computation.20 | convolution fusion | flops 339473920 | bytes 6957057 | tf_op jit(solution)/shard_map/gqd,kgd->gqk/dot_general | solution.py:40
  79.6 7.1 %collective-permute-done.6 = bf16[512,8,128]{2,0,1:T(8,128)(2,1)S(1)} collective-permute-done((bf16[512,8,128]{2,0,1:T(8,128)(2,1)}, bf16[512,8,128]{2,0,1:T(8,128)(2,1)S(1)}, u32[]{:S(2)}, u32[]{:S(2)}) %collective-permute-start.6) | collective-permute-done | bytes 1048608 | tf_op jit(solution)/shard_map/ppermute | solution.py:14
  86.8 0.9 fusion.9
  87.7 2.2 %fusion.20 = f32[8,320]{1,0:T(8,128)S(1)} fusion(f32[8,320,512]{2,1,0:T(8,128)S(1)} %get-tuple-element.25, f32[8,320]{1,0:T(8,128)S(1)} %get-tuple-element.15, s32[8,320]{1,0:T(8,128)S(1)} %add.92), kind=kLoop, calls=%fused_computation.32 | loop fusion | flops 7861760 | bytes 5273600 | tf_op jit(solution)/shard_map/reduce_sum | solution.py:46
  90.0 2.9 %fusion.11 = (f32[8,320]{1,0:T(8,128)S(1)}, f32[8,320]{1,0:T(8,128)S(1)}) fusion(f32[8,320,512]{2,1,0:T(8,128)S(1)} %get-tuple-element.23, f32[8,320]{1,0:T(8,128)S(1)} %get-tuple-element.13, pred[]{:T(512)S(6)} %ge.12, f32[8,320]{1,0:T(8,128)S(1)} %get-tuple-element.12, f32[8,320,512]{2,1,0:T(8,128)S(1)} %get-tuple-element.21, pred[]{:T(512)S(6)} %ge.13), kind=kLoop, calls=%fused_computation.23 | loop fusion | flops 13102080 | bytes 10526722 | tf_op jit(solution)/shard_map/reduce_sum | solution.py:46
  92.9 0.0 copy-start.2
  92.9 2.9 %fusion.15 = (f32[8,320]{1,0:T(8,128)S(1)}, f32[8,320]{1,0:T(8,128)S(1)}) fusion(f32[8,320,512]{2,1,0:T(8,128)S(1)} %get-tuple-element.19, f32[8,320]{1,0:T(8,128)S(1)} %get-tuple-element.11, pred[]{:T(512)S(6)} %ge.14, f32[8,320]{1,0:T(8,128)S(1)} %get-tuple-element.10, f32[8,320,512]{2,1,0:T(8,128)S(1)} %get-tuple-element.17, pred[]{:T(512)S(6)} %ge.15), kind=kLoop, calls=%fused_computation.27 | loop fusion | flops 13102080 | bytes 10526722 | tf_op jit(solution)/shard_map/reduce_sum | solution.py:46
  95.9 0.0 copy-done.2
  95.9 3.0 %fusion.40 = f32[8,320,128]{2,1,0:T(8,128)S(1)} fusion(f32[8,320,512]{2,1,0:T(8,128)S(1)} %get-tuple-element.25, f32[8,320]{1,0:T(8,128)S(1)} %get-tuple-element.15, s32[8,320]{1,0:T(8,128)S(1)} %add.92, f32[8,320]{1,0:T(8,128)S(1)} %get-tuple-element.9, f32[8,320]{1,0:T(8,128)S(1)} %get-tuple-element.14, bf16[512,8,128]{2,1,0:T(8,128)(2,1)S(1)} %copy-done.2), kind=kOutput, calls=%fused_computation.45 | convolution fusion | flops 344064000 | bytes 7643136 | tf_op jit(solution)/shard_map/gqk,kgd->gqd/dot_general | solution.py:47
  98.9 2.8 %fusion.46 = f32[8,320,128]{2,1,0:T(8,128)S(1)} fusion(f32[8,320,128]{2,1,0:T(8,128)S(1)} %fusion.40, bf16[512,8,128]{2,0,1:T(8,128)(2,1)} %collective-permute-done.1, f32[8,320,512]{2,1,0:T(8,128)S(1)} %get-tuple-element.23, f32[8,320]{1,0:T(8,128)S(1)} %get-tuple-element.13, pred[]{:T(512)S(6)} %ge.12, f32[8,320]{1,0:T(8,128)S(1)} %get-tuple-element.8), kind=kOutput, calls=%fused_computation.47 | convolution fusion | flops 342753280 | bytes 8933377 | tf_op jit(solution)/shard_map/gqk,kgd->gqd/dot_general | solution.py:47
  101.7 2.8 %fusion.52 = f32[8,320,128]{2,1,0:T(8,128)S(1)} fusion(f32[8,320,128]{2,1,0:T(8,128)S(1)} %fusion.46, bf16[512,8,128]{2,0,1:T(8,128)(2,1)} %collective-permute-done.3, f32[8,320,512]{2,1,0:T(8,128)S(1)} %get-tuple-element.21, f32[8,320]{1,0:T(8,128)S(1)} %get-tuple-element.12, pred[]{:T(512)S(6)} %ge.13, f32[8,320]{1,0:T(8,128)S(1)} %get-tuple-element.7), kind=kOutput, calls=%fused_computation.49 | convolution fusion | flops 342753280 | bytes 8933377 | tf_op jit(solution)/shard_map/gqk,kgd->gqd/dot_general | solution.py:47
  104.5 2.0 %fusion.58 = f32[8,320,128]{2,1,0:T(8,128)S(1)} fusion(f32[8,320,128]{2,1,0:T(8,128)S(1)} %fusion.52, bf16[512,8,128]{2,0,1:T(8,128)(2,1)S(1)} %collective-permute-done.5, f32[8,320,512]{2,1,0:T(8,128)S(1)} %get-tuple-element.19, f32[8,320]{1,0:T(8,128)S(1)} %get-tuple-element.11, pred[]{:T(512)S(6)} %ge.14, f32[8,320]{1,0:T(8,128)S(1)} %get-tuple-element.6), kind=kOutput, calls=%fused_computation.51 | convolution fusion | flops 342753280 | bytes 8933377 | tf_op jit(solution)/shard_map/gqk,kgd->gqd/dot_general | solution.py:47
  106.6 0.0 collective-permute-done.7
  106.6 2.0 %divide_convert_fusion = bf16[8,320,128]{2,1,0:T(8,128)(2,1)S(1)} fusion(f32[8,320,128]{2,1,0:T(8,128)S(1)} %fusion.58, bf16[512,8,128]{2,0,1:T(8,128)(2,1)S(1)} %collective-permute-done.7, f32[8,320,512]{2,1,0:T(8,128)S(1)} %get-tuple-element.17, f32[8,320]{1,0:T(8,128)S(1)} %get-tuple-element.10, pred[]{:T(512)S(6)} %ge.15, f32[8,320]{1,0:T(8,128)S(1)} %get-tuple-element.5), kind=kOutput, calls=%fused_computation.53 | convolution fusion | flops 343080960 | bytes 8278017 | tf_op jit(solution)/shard_map/gqk,kgd->gqd/dot_general | solution.py:47
  108.6 6.4 %fusion.64 = bf16[256,8,128]{2,1,0:T(8,128)(2,1)} fusion(bf16[2560,128]{1,0:T(8,128)(2,1)S(1)} %bitcast.41, s32[2048]{0:T(1024)S(1)} %bitcast_add_fusion), kind=kOutput, calls=%fused_computation.54 | convolution fusion | flops 1347682304 | bytes 1187840 | tf_op jit(solution)/shard_map/si,sd->id/dot_general | solution.py:91
  (6 shorter events, 0.1 us)
Async XLA Ops:
  0.0 53.1 %copy-start = (bf16[256,8,128]{2,1,0:T(8,128)(2,1)S(1)}, bf16[256,8,128]{2,1,0:T(8,128)(2,1)}, u32[]{:S(2)}) copy-start(bf16[256,8,128]{2,1,0:T(8,128)(2,1)} %param.4) | copy-start | bytes 1572868
  1.4 17.9 %collective-permute-start = (bf16[512,8,128]{2,0,1:T(8,128)(2,1)S(1)}, bf16[512,8,128]{2,0,1:T(8,128)(2,1)S(1)}, u32[]{:S(2)}, u32[]{:S(2)}) collective-permute-start(bf16[512,8,128]{2,0,1:T(8,128)(2,1)S(1)} %copy.11), channel_id=1, source_target_pairs={{0,1},{1,2},{2,3},{3,4},{4,5},{5,6},{6,7},{7,8},{8,9},{9,10},{10,1... | collective-permute-start | bytes 3145736 | tf_op jit(solution)/shard_map/ppermute | solution.py:14
  5.8 24.9 %collective-permute-start.1 = (bf16[512,8,128]{2,0,1:T(8,128)(2,1)}, bf16[512,8,128]{2,0,1:T(8,128)(2,1)}, u32[]{:S(2)}, u32[]{:S(2)}) collective-permute-start(bf16[512,8,128]{2,0,1:T(8,128)(2,1)} %copy.12), channel_id=1, source_target_pairs={{0,1},{1,2},{2,3},{3,4},{4,5},{5,6},{6,7},{7,8},{8,9},{9,10},{10,1... | collective-permute-start | bytes 3145736 | tf_op jit(solution)/shard_map/ppermute | solution.py:14
  19.3 22.5 %collective-permute-start.2 = (bf16[512,8,128]{2,0,1:T(8,128)(2,1)S(1)}, bf16[512,8,128]{2,0,1:T(8,128)(2,1)S(1)}, u32[]{:S(2)}, u32[]{:S(2)}) collective-permute-start(bf16[512,8,128]{2,0,1:T(8,128)(2,1)S(1)} %collective-permute-done), channel_id=1, source_target_pairs={{0,1},{1,2},{2,3},{3,4},{4,5},{5,6},{6,7},{7,8},{8,9},{9,10},{10,1... | collective-permute-start | bytes 3145736 | tf_op jit(solution)/shard_map/ppermute | solution.py:14
  30.7 26.2 %collective-permute-start.3 = (bf16[512,8,128]{2,0,1:T(8,128)(2,1)}, bf16[512,8,128]{2,0,1:T(8,128)(2,1)}, u32[]{:S(2)}, u32[]{:S(2)}) collective-permute-start(bf16[512,8,128]{2,0,1:T(8,128)(2,1)} %collective-permute-done.1), channel_id=1, source_target_pairs={{0,1},{1,2},{2,3},{3,4},{4,5},{5,6},{6,7},{7,8},{8,9},{9,10},{10,1... | collective-permute-start | bytes 3145736 | tf_op jit(solution)/shard_map/ppermute | solution.py:14
  41.8 22.6 %collective-permute-start.4 = (bf16[512,8,128]{2,0,1:T(8,128)(2,1)S(1)}, bf16[512,8,128]{2,0,1:T(8,128)(2,1)}, u32[]{:S(2)}, u32[]{:S(2)}) collective-permute-start(bf16[512,8,128]{2,0,1:T(8,128)(2,1)S(1)} %collective-permute-done.2), channel_id=1, source_target_pairs={{0,1},{1,2},{2,3},{3,4},{4,5},{5,6},{6,7},{7,8},{8,9},{9,10},{10,1... | collective-permute-start | bytes 3145736 | tf_op jit(solution)/shard_map/ppermute | solution.py:14
  53.1 5.7 %copy-start.1 = (bf16[512,8,128]{2,1,0:T(8,128)(2,1)S(1)}, bf16[512,8,128]{2,1,0:T(8,128)(2,1)}, u32[]{:S(2)}) copy-start(bf16[512,8,128]{2,1,0:T(8,128)(2,1)} %param.5) | copy-start | bytes 3145732
  56.9 18.7 %collective-permute-start.5 = (bf16[512,8,128]{2,0,1:T(8,128)(2,1)}, bf16[512,8,128]{2,0,1:T(8,128)(2,1)S(1)}, u32[]{:S(2)}, u32[]{:S(2)}) collective-permute-start(bf16[512,8,128]{2,0,1:T(8,128)(2,1)} %collective-permute-done.3), channel_id=1, source_target_pairs={{0,1},{1,2},{2,3},{3,4},{4,5},{5,6},{6,7},{7,8},{8,9},{9,10},{10,1... | collective-permute-start | bytes 3145736 | tf_op jit(solution)/shard_map/ppermute | solution.py:14
  64.4 22.4 %collective-permute-start.6 = (bf16[512,8,128]{2,0,1:T(8,128)(2,1)}, bf16[512,8,128]{2,0,1:T(8,128)(2,1)S(1)}, u32[]{:S(2)}, u32[]{:S(2)}) collective-permute-start(bf16[512,8,128]{2,0,1:T(8,128)(2,1)} %collective-permute-done.4), channel_id=1, source_target_pairs={{0,1},{1,2},{2,3},{3,4},{4,5},{5,6},{6,7},{7,8},{8,9},{9,10},{10,1... | collective-permute-start | bytes 3145736 | tf_op jit(solution)/shard_map/ppermute | solution.py:14
  75.5 31.0 %collective-permute-start.7 = (bf16[512,8,128]{2,0,1:T(8,128)(2,1)S(1)}, bf16[512,8,128]{2,0,1:T(8,128)(2,1)S(1)}, u32[]{:S(2)}, u32[]{:S(2)}) collective-permute-start(bf16[512,8,128]{2,0,1:T(8,128)(2,1)S(1)} %collective-permute-done.5), channel_id=1, source_target_pairs={{0,1},{1,2},{2,3},{3,4},{4,5},{5,6},{6,7},{7,8},{8,9},{9,10},{10,1... | collective-permute-start | bytes 3145736 | tf_op jit(solution)/shard_map/ppermute | solution.py:14
  92.9 3.0 %copy-start.2 = (bf16[512,8,128]{2,1,0:T(8,128)(2,1)S(1)}, bf16[512,8,128]{2,1,0:T(8,128)(2,1)}, u32[]{:S(2)}) copy-start(bf16[512,8,128]{2,1,0:T(8,128)(2,1)} %param.6) | copy-start | bytes 3145732
where the time goes:
time: 116 us; the launch traced here: 115 us
  waiting for transfers between devices  44.2 us (38%)
  matrix products  39.4 us (34%)
  starting transfers between devices  17.1 us (15%)
  other arithmetic  9.09 us (8%)
  local copies, waits for them, and re-layouts  5.07 us (4%)
    ppermute x8, waiting for transfers between devices, shifted(): return lax.ppermute(block, axis, route)  44.2 us
    ppermute x8, starting transfers between devices, shifted(): return lax.ppermute(block, axis, route)  17.1 us
    dot_general x5, matrix products, visit(): jnp.einsum('gqk,kgd->gqd', weights.astype(jnp.bfloat16), values_shard, pr...  12.6 us
    dot_general x1, matrix products, shards(): jnp.dot(placing.astype(jnp.float32), tokens_of, precision=lax.Precision.H...  9.23 us
    reduce_sum x3, other arithmetic, visit(): denominator = denominator * factor + jnp.sum(weights, axis=2)  8.1 us
    dot_general x5, matrix products, visit(): jnp.einsum('gqd,kgd->gqk', packed, keys_shard, preferred_element_type=jnp...  6.9 us
    dot_general x1, matrix products, shards(): jnp.einsum('si,sd->id', placing, finished.reshape(-1, width), preferred_e...  6.41 us
    unnamed x9, local copies, waits for them, and re-layouts  4.65 us
  transfers between devices with their start and end apart: 8, of which 6 were waited for; matrix products, arithmetic and copies ran while one was open for 38% of the time, Pallas kernels for 0%

commit v1 on v0

v1 whole, which is shorter than its diff:
```python
import functools
import math

import jax
import jax.numpy as jnp
from jax import lax
from jax.experimental import pallas as pl
from jax.experimental.pallas import tpu as pltpu
from jax.sharding import PartitionSpec as P

HEADS = 64
HOPS = 4
MOST = 40
LANES = 128
LOW = -1e30
MESH = pl.DeviceIdType.MESH


def dot(a, b):
    return lax.dot_general(a, b, (((1,), (0,)), ((), ())), preferred_element_type=jnp.float32)


def dot_t(a, b):
    return lax.dot_general(a, b, (((1,), (1,)), ((), ())), preferred_element_type=jnp.float32)


def pack_kernel(groups, capacity, q_ref, routes_ref, packed_ref, pos_ref, slots_ref, wide):
    tokens, routed, width = q_ref.shape
    per_group = HEADS // groups
    wide[...] = q_ref[...].astype(jnp.float32)
    lane = lax.broadcasted_iota(jnp.int32, (tokens, LANES), 1)
    group_of = routes_ref[...] // per_group
    hots = [(group_of[:, r : r + 1] == lane).astype(jnp.float32) for r in range(routed)]
    count = functools.reduce(jnp.add, hots)
    row = lax.broadcasted_iota(jnp.int32, (tokens, tokens), 0)
    col = lax.broadcasted_iota(jnp.int32, (tokens, tokens), 1)
    lower = (col < row).astype(jnp.bfloat16)
    rank = dot(lower, count.astype(jnp.bfloat16)) + (lane * capacity).astype(jnp.float32)
    slots = jnp.zeros((tokens, LANES), jnp.float32)
    for r in range(routed):
        slot = jnp.sum(hots[r] * rank, axis=1, keepdims=True)
        slots = jnp.where(lane == r, slot, slots)
        rank = rank + hots[r]
    slots_ref[...] = slots.astype(jnp.int32)
    slots_t = slots.T.astype(jnp.int32)
    token = lax.broadcasted_iota(jnp.int32, (tokens, width), 0).astype(jnp.bfloat16)
    rights = [
        jnp.concatenate([wide[:, r, :].astype(jnp.bfloat16), token], axis=1) for r in range(routed)
    ]
    step = 256
    total = groups * capacity
    place = lax.broadcasted_iota(jnp.int32, (step, tokens), 0)
    for at in range(0, total, step):
        acc = jnp.zeros((step, 2 * width), jnp.float32)
        for r in range(routed):
            here = (place == slots_t[r : r + 1, :] - at).astype(jnp.float32).astype(jnp.bfloat16)
            acc = acc + dot(here, rights[r])
        packed_ref[pl.ds(at, step), :] = acc[:, :width].astype(jnp.bfloat16)
        pos_ref[pl.ds(at, step), :] = acc[:, width:]


def unpack_kernel(fin_ref, slots_ref, out_ref, wide):
    tokens, routed, width = out_ref.shape
    total = fin_ref.shape[0]
    lane = lax.broadcasted_iota(jnp.int32, (tokens, 256), 1)
    for r in range(routed):
        slot = slots_ref[:, r : r + 1]
        acc = jnp.zeros((tokens, width), jnp.float32)
        for at in range(0, total, 256):
            here = (lane == slot - at).astype(jnp.float32).astype(jnp.bfloat16)
            acc = acc + dot(here, fin_ref[pl.ds(at, 256), :])
        wide[:, r, :] = acc
    out_ref[...] = wide[...].astype(jnp.bfloat16)


def remote(src, dst, send, recv, device):
    return pltpu.make_async_remote_copy(
        src_ref=src, dst_ref=dst, send_sem=send, recv_sem=recv,
        device_id=(device,), device_id_type=MESH,
    )


def attend(q, k, v, scale, mask=None):
    s = dot_t(q, k) * scale
    if mask is not None:
        s = mask(s)
    top = jnp.max(s, axis=1, keepdims=True)
    p = jnp.exp2(s - top).astype(jnp.bfloat16)
    ones = jnp.ones(v.shape, jnp.bfloat16)
    both = dot(p, jnp.concatenate([v, ones], axis=1))
    width = v.shape[1]
    total = both[:, width:]
    return both[:, :width] / total, top + jnp.log2(total)


def main_kernel(
    n, q, pos, k8, v8, fin, kh, vh, qb, qc, qd, oa, ob, oc, od, rb, rc, rd,
    st, ts, rs_b, rs_c, rs_d, kv_send, kv_recv, kv_local, qb_sem, qc_send, qc_recv,
    qd_send, qd_recv, ob_sem, oc_send, oc_recv, od_send, od_recv, sb_sem, sc_send, sc_recv,
    sd_send, sd_recv,
):
    groups, capacity, width = q.shape
    context = k8.shape[1]
    tokens = context // 2
    half = groups // 2
    chips = n // 2
    me = lax.axis_index("seq")
    c = me // 2
    k = me % 2
    other = 1 - k
    partner = c * 2 + other
    scale = jnp.float32(math.log2(math.e) / math.sqrt(width))
    exists = {-2: c >= 2, -1: c >= 1, 1: c + 1 < chips, 2: c + 2 < chips}

    barrier = pltpu.get_barrier_semaphore()

    def signal(device):
        pl.semaphore_signal(barrier, inc=1, device_id=(device,), device_id_type=MESH)

    signal(partner)
    for far, there in exists.items():
        @pl.when(there)
        def _(far=far):
            signal((c + far) * 2)
            signal((c + far) * 2 + 1)
    peers = 1
    for there in exists.values():
        peers = peers + 2 * there.astype(jnp.int32)
    pl.semaphore_wait(barrier, peers)

    def query_copy(x, s, r, far, g8):
        j, g = g8 // half, g8 % half
        return remote(q.at[g8], x.at[k, g], s.at[g8], r.at[k, g], (c - far) * 2 + j)

    order = [j * half + g for g in range(half) for j in range(2)]
    for g8 in order:
        @pl.when(exists[-1])
        def _(g8=g8):
            query_copy(qc, qc_send, qc_recv, 1, g8).start()
        @pl.when(exists[-2])
        def _(g8=g8):
            query_copy(qd, qd_send, qd_recv, 2, g8).start()

    def kv_copies():
        return [
            remote(a.at[pl.ds(other * half, half)], b.at[k], kv_send.at[i], kv_recv.at[i], partner)
            for i, (a, b) in enumerate(((k8, kh), (v8, vh)))
        ]

    def kv_locals():
        return [
            pltpu.make_async_copy(a.at[pl.ds(k * half, half)], b.at[k], kv_local.at[i])
            for i, (a, b) in enumerate(((k8, kh), (v8, vh)))
        ]

    for one in kv_copies() + kv_locals():
        one.start()

    def qb_copy():
        return remote(q.at[pl.ds(0, half)], qb, qb_sem.at[0], qb_sem.at[1], partner)

    @pl.when(k == 1)
    def _():
        qb_copy().start()

    lane = lax.broadcasted_iota(jnp.int32, (capacity, LANES), 1)

    def keep(at, i, lse):
        st[at, pl.ds(0, capacity), :] = jnp.where(lane == i, lse, st[at, pl.ds(0, capacity), :])

    st[...] = jnp.full(st.shape, LOW, jnp.float32)

    column = lax.broadcasted_iota(jnp.int32, (capacity, tokens), 1).astype(jnp.float32)

    def own(g, carry):
        at = pos[g]
        limit = jnp.concatenate([at] * (tokens // LANES), axis=1)

        def mask(s):
            tail = jnp.where(column <= limit, s[:, context - tokens :], jnp.float32(LOW))
            return jnp.concatenate([s[:, : context - tokens], tail], axis=1)

        o, lse = attend(q[g], k8[g], v8[g], scale, mask)
        oa[g] = o
        keep(0, g, lse)
        return carry

    lax.fori_loop(0, groups, own, 0)

    for one in kv_copies():
        one.wait_recv()
    for one in kv_locals():
        one.wait()

    def stat_copies(slot, i, r, s_sem, r_sem, device):
        return remote(ts.at[slot], r.at[i], s_sem, r_sem, device)

    def second(queries, at):
        def body(g, carry):
            o, lse = attend(queries(g), kh[0, g], vh[0, g], scale)
            ob[g] = o.astype(jnp.bfloat16)
            keep(1, at + g, lse)
            return carry
        lax.fori_loop(0, half, body, 0)

    def ob_copies():
        return [
            remote(ob, rb, ob_sem.at[0], ob_sem.at[1], partner),
            remote(ts.at[0], rs_b, sb_sem.at[0], sb_sem.at[1], partner),
        ]

    @pl.when(k == 0)
    def _():
        qb_copy().wait_recv()
        second(lambda g: qb[g], 0)
        ts[0] = st[1].T[:8]
        for one in ob_copies():
            one.start()

    @pl.when(k == 1)
    def _():
        second(lambda g: q[half + g], half)

    def out_copy(o, r, s_sem, r_sem, far, j, g):
        return remote(o.at[j, g], r.at[k * half + g], s_sem.at[j, g], r_sem.at[k * half + g], (c + far) * 2 + j)

    def stat_copy(slot, r, s_sem, r_sem, far, j):
        return remote(ts.at[slot + j], r.at[k], s_sem.at[j], r_sem.at[k], (c + far) * 2 + j)

    def serve(far, j, g, x, x_send, x_recv, o, o_send, r, r_recv, at, part):
        remote(x.at[j, g], x.at[j, g], x_send.at[0], x_recv.at[j, g], partner).wait_recv()
        if part:
            keys, values = kh[1, g], vh[1, g]
        else:
            keys = jnp.concatenate([kh[0, g], kh[1, g]], axis=0)
            values = jnp.concatenate([vh[0, g], vh[1, g]], axis=0)
        out, lse = attend(x[j, g], keys, values, scale)
        o[j, g] = out.astype(jnp.bfloat16)
        keep(at, g, lse)
        out_copy(o, r, o_send, r_recv, far, j, g).start()

    @pl.when(exists[1])
    def _():
        def body(i, carry):
            g, j = i // 2, i % 2
            serve(1, j, g, qc, qc_send, qc_recv, oc, oc_send, rc, oc_recv, 2 + j, False)
            return carry
        lax.fori_loop(0, groups, body, 0)
        for j in range(2):
            ts[1 + j] = st[2 + j].T[:8]
            stat_copy(1, rs_c, sc_send, sc_recv, 1, j).start()

    @pl.when(exists[2])
    def _():
        def body(g, carry):
            for j in range(2):
                serve(2, j, g, qd, qd_send, qd_recv, od, od_send, rd, od_recv, 4 + j, j == 1)
            return carry
        lax.fori_loop(0, half, body, 0)
        for j in range(2):
            ts[3 + j] = st[4 + j].T[:8]
            stat_copy(3, rs_d, sd_send, sd_recv, 2, j).start()

    for far, r, rs, r_recv, s_recv, o, o_send, s_send in (
        (1, rc, rs_c, oc_recv, sc_recv, oc, oc_send, sc_send),
        (2, rd, rs_d, od_recv, sd_recv, od, od_send, sd_send),
    ):
        @pl.when(exists[-far])
        def _(r=r, rs=rs, r_recv=r_recv, s_recv=s_recv, o=o, o_send=o_send, s_send=s_send):
            for g8 in range(groups):
                remote(o.at[0, 0], r.at[g8], o_send.at[0, 0], r_recv.at[g8], partner).wait_recv()
            for j in range(2):
                remote(ts.at[0], rs.at[j], s_send.at[0], s_recv.at[j], partner).wait_recv()

        @pl.when(jnp.logical_not(exists[-far]))
        def _(r=r, rs=rs):
            r[...] = jnp.zeros(r.shape, r.dtype)
            rs[...] = jnp.full(rs.shape, LOW, rs.dtype)

    @pl.when(k == 1)
    def _():
        for one in ob_copies():
            one.wait_recv()

    @pl.when(k == 0)
    def _():
        rb[...] = jnp.zeros(rb.shape, rb.dtype)
        rs_b[...] = jnp.full(rs_b.shape, LOW, rs_b.dtype)

    padded = st.shape[1]
    for h in range(2):
        tiles = [rs_c[h], rs_d[h]] + ([rs_b[...]] if h == 0 else [])
        pad = jnp.full((LANES - 8 * len(tiles), padded), LOW, jnp.float32)
        turned = jnp.concatenate(tiles + [pad], axis=0).T
        for g in range(half):
            g8 = h * half + g
            lse_a = st[0, pl.ds(0, capacity), g8 : g8 + 1]
            lse_c = turned[:capacity, g : g + 1]
            lse_d = turned[:capacity, 8 + g : 9 + g]
            if h == 0:
                lse_b = turned[:capacity, 16 + g : 17 + g]
                o_b = rb[g].astype(jnp.float32)
            else:
                kept = st[1, pl.ds(0, capacity), g8 : g8 + 1]
                lse_b = jnp.where(k == 1, kept, jnp.float32(LOW))
                o_b = ob[g].astype(jnp.float32)
            top = jnp.maximum(jnp.maximum(lse_a, lse_b), jnp.maximum(lse_c, lse_d))
            w_a, w_b, w_c, w_d = (jnp.exp2(x - top) for x in (lse_a, lse_b, lse_c, lse_d))
            inverse = 1.0 / (w_a + w_b + w_c + w_d)
            merged = (
                oa[g8] * (w_a * inverse)
                + o_b * (w_b * inverse)
                + rc[g8].astype(jnp.float32) * (w_c * inverse)
                + rd[g8].astype(jnp.float32) * (w_d * inverse)
            )
            fin[g8] = merged.astype(jnp.bfloat16)

    for one in kv_copies():
        one.wait_send()

    @pl.when(k == 1)
    def _():
        qb_copy().wait_send()

    @pl.when(k == 0)
    def _():
        for one in ob_copies():
            one.wait_send()

    for far, x, s, r in ((1, qc, qc_send, qc_recv), (2, qd, qd_send, qd_recv)):
        @pl.when(exists[-far])
        def _(far=far, x=x, s=s, r=r):
            for g8 in range(groups):
                query_copy(x, s, r, far, g8).wait_send()

    for far, o, r, o_send, r_recv, slot, rs, s_send, s_recv in (
        (1, oc, rc, oc_send, oc_recv, 1, rs_c, sc_send, sc_recv),
        (2, od, rd, od_send, od_recv, 3, rs_d, sd_send, sd_recv),
    ):
        @pl.when(exists[far])
        def _(far=far, o=o, r=r, o_send=o_send, r_recv=r_recv, slot=slot, rs=rs, s_send=s_send, s_recv=s_recv):
            for j in range(2):
                for g in range(half):
                    out_copy(o, r, o_send, r_recv, far, j, g).wait_send()
                stat_copy(slot, rs, s_send, s_recv, far, j).wait_send()


def shards(n, queries, keys, values, routes):
    tokens, routed, width = queries.shape
    context, groups, _ = keys.shape
    capacity = HEADS // groups * MOST
    half = groups // 2
    padded = -(-capacity // LANES) * LANES
    total = groups * capacity
    vmem = pl.BlockSpec(memory_space=pltpu.VMEM)
    packed, pos, slots = pl.pallas_call(
        functools.partial(pack_kernel, groups, capacity),
        out_shape=(
            jax.ShapeDtypeStruct((total, width), jnp.bfloat16),
            jax.ShapeDtypeStruct((total, width), jnp.float32),
            jax.ShapeDtypeStruct((tokens, LANES), jnp.int32),
        ),
        in_specs=[vmem] * 2,
        out_specs=(vmem,) * 3,
        scratch_shapes=[pltpu.VMEM((tokens, routed, width), jnp.float32)],
        name="pack",
    )(queries, routes)
    k8 = keys.transpose(1, 0, 2)
    v8 = values.transpose(1, 0, 2)
    bf = lambda *shape: pltpu.VMEM(shape, jnp.bfloat16)
    f32 = lambda *shape: pltpu.VMEM(shape, jnp.float32)
    sem = lambda *shape: pltpu.SemaphoreType.DMA(shape)
    fin = pl.pallas_call(
        functools.partial(main_kernel, n),
        out_shape=jax.ShapeDtypeStruct((groups, capacity, width), jnp.bfloat16),
        in_specs=[vmem] * 4,
        out_specs=vmem,
        scratch_shapes=[
            bf(2, half, context, width),
            bf(2, half, context, width),
            bf(half, capacity, width),
            bf(2, half, capacity, width),
            bf(2, half, capacity, width),
            f32(groups, capacity, width),
            bf(half, capacity, width),
            bf(2, half, capacity, width),
            bf(2, half, capacity, width),
            bf(half, capacity, width),
            bf(groups, capacity, width),
            bf(groups, capacity, width),
            f32(6, padded, LANES),
            f32(5, 8, padded),
            f32(8, padded),
            f32(2, 8, padded),
            f32(2, 8, padded),
            sem(2), sem(2), sem(2), sem(2),
            sem(groups), sem(2, half), sem(groups), sem(2, half),
            sem(2), sem(2, half), sem(groups), sem(2, half), sem(groups),
            sem(2), sem(2), sem(2), sem(2), sem(2),
        ],
        compiler_params=pltpu.CompilerParams(
            collective_id=0, has_side_effects=True, vmem_limit_bytes=60 * 1024 * 1024
        ),
        name="main",
    )(packed.reshape(groups, capacity, width), pos.reshape(groups, capacity, width), k8, v8)
    return pl.pallas_call(
        unpack_kernel,
        out_shape=jax.ShapeDtypeStruct((tokens, routed, width), jnp.bfloat16),
        in_specs=[vmem] * 2,
        out_specs=vmem,
        scratch_shapes=[pltpu.VMEM((tokens, routed, width), jnp.float32)],
        name="unpack",
    )(fin.reshape(total, width), slots)


def solution(mesh):
    n = mesh.shape["seq"]
    placed = (P("seq", None, None), P("seq", None, None), P("seq", None, None), P("seq", None))
    return jax.shard_map(
        functools.partial(shards, n),
        mesh=mesh,
        in_specs=placed,
        out_specs=P("seq", None, None),
        check_vma=False,
    )
```

time: 116 us -> 81.2 us (0.70)
  the two profiles are of different devices: /device:TPU:16 before, /device:TPU:21 now
where the time goes in v1:
time: 81.2 us; the launch traced here: 80.9 us
  Pallas kernels  76.2 us (94%)
  local copies, waits for them, and re-layouts  4.71 us (6%)
    pallas_call x1, Pallas kernels, shards(): pl.pallas_call(functools.partial(main_kernel, n), out_shape=jax.ShapeDtyp...  63.9 us
    pallas_call x1, Pallas kernels, shards(): pl.pallas_call(functools.partial(pack_kernel, groups, capacity), out_shap...  6.99 us
    pallas_call x1, Pallas kernels, shards(): pl.pallas_call(unpack_kernel, out_shape=jax.ShapeDtypeStruct((tokens, rou...  5.36 us
    transpose x1, local copies, waits for them, and re-layouts, shards(): v8 = values.transpose(1, 0, 2)  3.23 us

profile of v1, /device:TPU:21, one launch (start us, length us, event | category | flops | bytes accessed | tf_op | source)
XLA Modules:
  0.0 80.9 jit_solution(10179964316744166524)
XLA Ops:
  0.0 1.5 %copy.5.routes_ref = s32[256,8]{1,0:T(8,128)} copy(s32[256,8]{0,1:T(8,128)} %param.7) | data formatting | bytes 16384 | tf_op args[3]
  1.5 7.0 %pack.1 = (bf16[2560,128]{1,0:T(8,128)(2,1)}, f32[2560,128]{1,0:T(8,128)}, s32[256,128]{1,0:T(8,128)}) custom-call(bf16[256,8,128]{2,1,0:T(8,128)(2,1)} %q_ref.1, s32[256,8]{1,0:T(8,128)} %copy.5.routes_ref), custom_call_target="tpu_custom_call" | custom-call | tf_op jit(solution)/shard_map/pack/pallas_call | solution.py:356
  8.5 3.2 %copy_bitcast_fusion = (bf16[8,512,128]{2,1,0:T(8,128)(2,1)}, bf16[8,512,128]{2,1,0:T(8,128)(2,1)}) fusion(bf16[512,8,128]{2,1,0:T(8,128)(2,1)} %param.6, bf16[512,8,128]{2,1,0:T(8,128)(2,1)} %param.5), kind=kLoop, calls=%fused_computation | loop fusion | bytes 4194304 | tf_op jit(solution)/shard_map/transpose | solution.py:369
  11.7 63.9 %main.1 = bf16[8,320,128]{2,1,0:T(8,128)(2,1)} custom-call(bf16[8,320,128]{2,1,0:T(8,128)(2,1)} %bitcast.9, f32[8,320,128]{2,1,0:T(8,128)} %bitcast.8, bf16[8,512,128]{2,1,0:T(8,128)(2,1)} %get-tuple-element.12.k8, bf16[8,512,128]{2,1,0:T(8,128)(2,1)} %get-tuple-element.11.v8), custom_call_target="tpu_custom_call" | custom-call | tf_op jit(solution)/shard_map/main/pallas_call | solution.py:373
  75.6 5.4 %unpack.1 = bf16[256,8,128]{2,1,0:T(8,128)(2,1)} custom-call(bf16[2560,128]{1,0:T(8,128)(2,1)} %bitcast.7, s32[256,128]{1,0:T(8,128)} %get-tuple-element.10.slots_ref), custom_call_target="tpu_custom_call" | custom-call | tf_op jit(solution)/shard_map/unpack/pallas_call | solution.py:406

commit v2 on v1

v2 whole, which is shorter than its diff:
```python
import functools
import math

import jax
import jax.numpy as jnp
from jax import lax
from jax.experimental import pallas as pl
from jax.experimental.pallas import tpu as pltpu
from jax.sharding import PartitionSpec as P

HEADS = 64
HOPS = 4
MOST = 40
LANES = 128
LOW = -1e30
MESH = pl.DeviceIdType.MESH


def dot(a, b):
    return lax.dot_general(a, b, (((1,), (0,)), ((), ())), preferred_element_type=jnp.float32)


def dot_t(a, b):
    return lax.dot_general(a, b, (((1,), (1,)), ((), ())), preferred_element_type=jnp.float32)


def pack_kernel(groups, capacity, q_ref, routes_ref, packed_ref, pos_ref, slots_ref, wide):
    tokens, routed, width = q_ref.shape
    per_group = HEADS // groups
    wide[...] = q_ref[...].astype(jnp.float32)
    lane = lax.broadcasted_iota(jnp.int32, (tokens, LANES), 1)
    turned = routes_ref[...].astype(jnp.float32)
    group_of = jnp.concatenate([turned] * (LANES // routed), axis=0).T.astype(jnp.int32) // per_group
    hots = [(group_of[:, r : r + 1] == lane).astype(jnp.float32) for r in range(routed)]
    count = functools.reduce(jnp.add, hots)
    row = lax.broadcasted_iota(jnp.int32, (tokens, tokens), 0)
    col = lax.broadcasted_iota(jnp.int32, (tokens, tokens), 1)
    lower = (col < row).astype(jnp.bfloat16)
    rank = dot(lower, count.astype(jnp.bfloat16)) + (lane * capacity).astype(jnp.float32)
    slots = jnp.zeros((tokens, LANES), jnp.float32)
    for r in range(routed):
        slot = jnp.sum(hots[r] * rank, axis=1, keepdims=True)
        slots = jnp.where(lane == r, slot, slots)
        rank = rank + hots[r]
    slots_ref[...] = slots.astype(jnp.int32)
    slots_t = slots.T.astype(jnp.int32)
    token = lax.broadcasted_iota(jnp.int32, (tokens, width), 0).astype(jnp.bfloat16)
    rights = [
        jnp.concatenate([wide[:, r, :].astype(jnp.bfloat16), token], axis=1) for r in range(routed)
    ]
    step = 256
    total = groups * capacity
    place = lax.broadcasted_iota(jnp.int32, (step, tokens), 0)
    for at in range(0, total, step):
        acc = jnp.zeros((step, 2 * width), jnp.float32)
        for r in range(routed):
            here = (place == slots_t[r : r + 1, :] - at).astype(jnp.float32).astype(jnp.bfloat16)
            acc = acc + dot(here, rights[r])
        packed_ref[pl.ds(at, step), :] = acc[:, :width].astype(jnp.bfloat16)
        pos_ref[pl.ds(at, step), :] = acc[:, width:]


def unpack_kernel(fin_ref, slots_ref, out_ref, wide):
    tokens, routed, width = out_ref.shape
    total = fin_ref.shape[0]
    lane = lax.broadcasted_iota(jnp.int32, (tokens, 256), 1)
    for r in range(routed):
        slot = slots_ref[:, r : r + 1]
        acc = jnp.zeros((tokens, width), jnp.float32)
        for at in range(0, total, 256):
            here = (lane == slot - at).astype(jnp.float32).astype(jnp.bfloat16)
            acc = acc + dot(here, fin_ref[pl.ds(at, 256), :])
        wide[:, r, :] = acc
    out_ref[...] = wide[...].astype(jnp.bfloat16)


def remote(src, dst, send, recv, device):
    return pltpu.make_async_remote_copy(
        src_ref=src, dst_ref=dst, send_sem=send, recv_sem=recv,
        device_id=(device,), device_id_type=MESH,
    )


def attend(q, k, v, scale, mask=None):
    s = dot_t(q, k) * scale
    if mask is not None:
        s = mask(s)
    top = jnp.max(s, axis=1, keepdims=True)
    p = jnp.exp2(s - top).astype(jnp.bfloat16)
    ones = jnp.ones(v.shape, jnp.bfloat16)
    both = dot(p, jnp.concatenate([v, ones], axis=1))
    width = v.shape[1]
    total = both[:, width:]
    return both[:, :width] / total, top + jnp.log2(total)


def squeeze(lse, padded):
    rows = lse.shape[0]
    return jnp.concatenate([lse, jnp.zeros((padded - rows, LANES), jnp.float32)], axis=0).T[:8]


def widen(tile, rows):
    return jnp.concatenate([tile] * (LANES // 8), axis=0).T[:rows]


def merge(parts):
    top = functools.reduce(jnp.maximum, [lse for _, lse in parts])
    weights = [jnp.exp2(lse - top) for _, lse in parts]
    total = functools.reduce(jnp.add, weights)
    mixed = functools.reduce(jnp.add, [o.astype(jnp.float32) * w for (o, _), w in zip(parts, weights)])
    return mixed / total, top + jnp.log2(total)


def main_kernel(
    n, q, pos, k8, v8, fin, kh, vh, qb, qc, qd, oa, la, ob, lb, tb, rb, sb,
    oc, tc, od, ld, td, rx, sx, rc, sc, rd, sd,
    kv_send, kv_recv, kv_local, qb_sem, qc_send, qc_recv, qd_send, qd_recv, relay_send,
    ob_send, ob_recv, tb_send, tb_recv, oc_send, tc_send, od_send, td_send,
    rx_recv, sx_recv, rc_recv, sc_recv, rd_recv, sd_recv,
):
    groups, capacity, width = q.shape
    context = k8.shape[1]
    tokens = context // 2
    padded = tb.shape[2]
    half = groups // 2
    chips = n // 2
    me = lax.axis_index("seq")
    c = me // 2
    k = me % 2
    other = 1 - k
    partner = c * 2 + other
    even = c % 2 == 0
    odd = c % 2 == 1
    scale = jnp.float32(math.log2(math.e) / math.sqrt(width))
    exists = {-2: c >= 2, -1: c >= 1, 1: c + 1 < chips, 2: c + 2 < chips}
    near = jnp.logical_and(odd, exists[-1])

    barrier = pltpu.get_barrier_semaphore()

    def signal(device):
        pl.semaphore_signal(barrier, inc=1, device_id=(device,), device_id_type=MESH)

    signal(partner)
    peers = 1
    for far, there in exists.items():
        @pl.when(there)
        def _(far=far):
            signal((c + far) * 2)
            signal((c + far) * 2 + 1)
        peers = peers + 2 * there.astype(jnp.int32)
    pl.semaphore_wait(barrier, peers)

    def query_copy(x, s, r, far, g8):
        j, g = g8 // half, g8 % half
        return remote(q.at[g8], x.at[k, g], s.at[g8], r.at[k, g], (c - far) * 2 + j)

    for g8 in [j * half + g for g in range(half) for j in range(2)]:
        @pl.when(exists[-2])
        def _(g8=g8):
            query_copy(qd, qd_send, qd_recv, 2, g8).start()
        @pl.when(near)
        def _(g8=g8):
            query_copy(qc, qc_send, qc_recv, 1, g8).start()

    def kv_copies():
        return [
            remote(a.at[pl.ds(other * half, half)], b.at[k], kv_send.at[i], kv_recv.at[i], partner)
            for i, (a, b) in enumerate(((k8, kh), (v8, vh)))
        ]

    def kv_locals():
        return [
            pltpu.make_async_copy(a.at[pl.ds(k * half, half)], b.at[k], kv_local.at[i])
            for i, (a, b) in enumerate(((k8, kh), (v8, vh)))
        ]

    for one in kv_copies() + kv_locals():
        one.start()

    def qb_copy():
        return remote(q.at[pl.ds(0, half)], qb, qb_sem.at[0], qb_sem.at[1], partner)

    @pl.when(k == 1)
    def _():
        qb_copy().start()

    column = lax.broadcasted_iota(jnp.int32, (capacity, tokens), 1).astype(jnp.float32)

    def own(g, carry):
        limit = jnp.concatenate([pos[g]] * (tokens // LANES), axis=1)

        def mask(s):
            tail = jnp.where(column <= limit, s[:, context - tokens :], jnp.float32(LOW))
            return jnp.concatenate([s[:, : context - tokens], tail], axis=1)

        oa[g], la[g] = attend(q[g], k8[g], v8[g], scale, mask)
        return carry

    lax.fori_loop(0, groups, own, 0)

    for one in kv_copies():
        one.wait_recv()
    for one in kv_locals():
        one.wait()

    @pl.when(k == 0)
    def _():
        qb_copy().wait_recv()

    def b_copies(g):
        return (
            remote(ob.at[g], rb.at[g], ob_send.at[g], ob_recv.at[g], partner),
            remote(tb.at[g], sb.at[g], tb_send.at[g], tb_recv.at[g], partner),
        )

    def c_near(j, g):
        at = k * half + g
        to = (c + 1) * 2 + j
        return (
            remote(oc.at[j, g], rc.at[at], oc_send.at[j, g], rc_recv.at[at], to),
            remote(tc.at[j, g], sc.at[at], tc_send.at[j, g], sc_recv.at[at], to),
        )

    def c_relay(j, g):
        to = (c - 1) * 2 + k
        return (
            remote(oc.at[j, g], rx.at[j, g], oc_send.at[j, g], rx_recv.at[j, g], to),
            remote(tc.at[j, g], sx.at[j, g], tc_send.at[j, g], sx_recv.at[j, g], to),
        )

    def d_copies(j, g):
        at = k * half + g
        to = (c + 2) * 2 + j
        return (
            remote(od.at[j, g], rd.at[at], od_send.at[j, g], rd_recv.at[at], to),
            remote(td.at[j, g], sd.at[at], td_send.at[j, g], sd_recv.at[at], to),
        )

    def query_relay(j, g):
        return remote(
            qd.at[j, g], qc.at[j, g], relay_send.at[j, g], qc_recv.at[j, g], (c + 1) * 2 + k
        )

    def start(copies):
        for one in copies:
            one.start()

    def both(x, g):
        return jnp.concatenate([x[0, g], x[1, g]], axis=0)

    lag, delay = 1, 3

    def step(i, carry):
        @pl.when(jnp.logical_and(i < groups, exists[2]))
        def _():
            g, j = i // 2, i % 2
            remote(qd.at[j, g], qd.at[j, g], qd_send.at[0], qd_recv.at[j, g], partner).wait_recv()

            @pl.when(even)
            def _():
                query_relay(j, g).start()

            def put(out, lse):
                od[j, g] = out.astype(jnp.bfloat16)
                ld[j, g] = lse

            @pl.when(j == 0)
            def _():
                put(*attend(qd[j, g], both(kh, g), both(vh, g), scale))

            @pl.when(j == 1)
            def _():
                put(*attend(qd[j, g], kh[1, g], vh[1, g], scale))

            @pl.when(odd)
            def _():
                td[j, g] = squeeze(ld[j, g], padded)
                start(d_copies(j, g))

        @pl.when(i < half)
        def _():
            @pl.when(k == 1)
            def _():
                qb[i] = q[half + i]

            out, lse = attend(qb[i], kh[0, i], vh[0, i], scale)
            ob[i] = out.astype(jnp.bfloat16)
            lb[i] = lse

            @pl.when(k == 0)
            def _():
                tb[i] = squeeze(lse, padded)
                start(b_copies(i))

        @pl.when(jnp.logical_and(jnp.logical_and(i >= lag, i < groups + lag), exists[1]))
        def _():
            at = i - lag
            g, j = at // 2, at % 2
            remote(qc.at[j, g], qc.at[j, g], qc_send.at[0], qc_recv.at[j, g], partner).wait_recv()
            out, lse = attend(qc[j, g], both(kh, g), both(vh, g), scale)
            oc[j, g] = out.astype(jnp.bfloat16)
            tc[j, g] = squeeze(lse, padded)

            @pl.when(even)
            def _():
                start(c_near(j, g))

            @pl.when(odd)
            def _():
                start(c_relay(j, g))

        @pl.when(jnp.logical_and(jnp.logical_and(i >= delay, even), exists[2]))
        def _():
            at = i - delay
            g, j = at // 2, at % 2
            remote(oc.at[j, g], rx.at[j, g], oc_send.at[j, g], rx_recv.at[j, g], partner).wait_recv()
            remote(tc.at[j, g], sx.at[j, g], tc_send.at[j, g], sx_recv.at[j, g], partner).wait_recv()
            out, lse = merge([(od[j, g], ld[j, g]), (rx[j, g], widen(sx[j, g], capacity))])
            od[j, g] = out.astype(jnp.bfloat16)
            td[j, g] = squeeze(lse, padded)
            start(d_copies(j, g))

        return carry

    lax.fori_loop(0, groups + delay, step, 0)

    def absent(o, t):
        o[...] = jnp.zeros(o.shape, o.dtype)
        t[...] = jnp.full(t.shape, LOW, t.dtype)

    @pl.when(jnp.logical_not(near))
    def _():
        absent(rc, sc)

    @pl.when(jnp.logical_not(exists[-2]))
    def _():
        absent(rd, sd)

    @pl.when(k == 0)
    def _():
        absent(rb, sb)

    def finish(g8, carry):
        @pl.when(near)
        def _():
            remote(oc.at[0, 0], rc.at[g8], oc_send.at[0, 0], rc_recv.at[g8], partner).wait_recv()
            remote(tc.at[0, 0], sc.at[g8], tc_send.at[0, 0], sc_recv.at[g8], partner).wait_recv()

        @pl.when(exists[-2])
        def _():
            remote(od.at[0, 0], rd.at[g8], od_send.at[0, 0], rd_recv.at[g8], partner).wait_recv()
            remote(td.at[0, 0], sd.at[g8], td_send.at[0, 0], sd_recv.at[g8], partner).wait_recv()

        parts = [
            (oa[g8], la[g8]), (rc[g8], widen(sc[g8], capacity)), (rd[g8], widen(sd[g8], capacity))
        ]
        second = jnp.logical_and(k == 1, g8 < half)

        @pl.when(second)
        def _():
            for one in b_copies(g8 % half):
                one.wait_recv()
            g = g8 % half
            fin[g8] = merge(parts + [(rb[g], widen(sb[g], capacity))])[0].astype(jnp.bfloat16)

        @pl.when(jnp.logical_not(second))
        def _():
            g = g8 % half
            lse = jnp.where(k == 1, lb[g], jnp.float32(LOW))
            fin[g8] = merge(parts + [(ob[g], lse)])[0].astype(jnp.bfloat16)

        return carry

    lax.fori_loop(0, groups, finish, 0)

    for one in kv_copies():
        one.wait_send()

    @pl.when(k == 1)
    def _():
        qb_copy().wait_send()

    def sent(there, make):
        @pl.when(there)
        def _():
            for j in range(2):
                for g in range(half):
                    for one in make(j, g):
                        one.wait_send()

    @pl.when(k == 0)
    def _():
        for g in range(half):
            for one in b_copies(g):
                one.wait_send()

    sent(exists[-2], lambda j, g: (query_copy(qd, qd_send, qd_recv, 2, j * half + g),))
    sent(near, lambda j, g: (query_copy(qc, qc_send, qc_recv, 1, j * half + g),))
    sent(jnp.logical_and(even, exists[2]), lambda j, g: (query_relay(j, g),))
    sent(exists[2], d_copies)
    sent(jnp.logical_and(even, exists[1]), c_near)
    sent(jnp.logical_and(odd, exists[1]), c_relay)


def shards(n, queries, keys, values, routes):
    tokens, routed, width = queries.shape
    context, groups, _ = keys.shape
    capacity = HEADS // groups * MOST
    half = groups // 2
    padded = -(-capacity // LANES) * LANES
    total = groups * capacity
    vmem = pl.BlockSpec(memory_space=pltpu.VMEM)
    packed, pos, slots = pl.pallas_call(
        functools.partial(pack_kernel, groups, capacity),
        out_shape=(
            jax.ShapeDtypeStruct((total, width), jnp.bfloat16),
            jax.ShapeDtypeStruct((total, width), jnp.float32),
            jax.ShapeDtypeStruct((tokens, LANES), jnp.int32),
        ),
        in_specs=[vmem] * 2,
        out_specs=(vmem,) * 3,
        scratch_shapes=[pltpu.VMEM((tokens, routed, width), jnp.float32)],
        name="pack",
    )(queries, routes.T)
    k8 = keys.transpose(1, 0, 2)
    v8 = values.transpose(1, 0, 2)
    bf = lambda *shape: pltpu.VMEM(shape, jnp.bfloat16)
    f32 = lambda *shape: pltpu.VMEM(shape, jnp.float32)
    sem = lambda *shape: pltpu.SemaphoreType.DMA(shape)
    chunks = lambda: bf(2, half, capacity, width)
    fin = pl.pallas_call(
        functools.partial(main_kernel, n),
        out_shape=jax.ShapeDtypeStruct((groups, capacity, width), jnp.bfloat16),
        in_specs=[vmem] * 4,
        out_specs=vmem,
        scratch_shapes=[
            bf(2, half, context, width), bf(2, half, context, width),
            bf(half, capacity, width), chunks(), chunks(),
            f32(groups, capacity, width), f32(groups, capacity, width),
            bf(half, capacity, width), f32(half, capacity, width), f32(half, 8, padded),
            bf(half, capacity, width), f32(half, 8, padded),
            chunks(), f32(2, half, 8, padded),
            chunks(), f32(2, half, capacity, width), f32(2, half, 8, padded),
            chunks(), f32(2, half, 8, padded),
            bf(groups, capacity, width), f32(groups, 8, padded),
            bf(groups, capacity, width), f32(groups, 8, padded),
            sem(2), sem(2), sem(2), sem(2),
            sem(groups), sem(2, half), sem(groups), sem(2, half), sem(2, half),
            sem(half), sem(half), sem(half), sem(half),
            sem(2, half), sem(2, half), sem(2, half), sem(2, half),
            sem(2, half), sem(2, half), sem(groups), sem(groups), sem(groups), sem(groups),
        ],
        compiler_params=pltpu.CompilerParams(
            collective_id=0, has_side_effects=True, vmem_limit_bytes=60 * 1024 * 1024
        ),
        name="main",
    )(packed.reshape(groups, capacity, width), pos.reshape(groups, capacity, width), k8, v8)
    return pl.pallas_call(
        unpack_kernel,
        out_shape=jax.ShapeDtypeStruct((tokens, routed, width), jnp.bfloat16),
        in_specs=[vmem] * 2,
        out_specs=vmem,
        scratch_shapes=[pltpu.VMEM((tokens, routed, width), jnp.float32)],
        name="unpack",
    )(fin.reshape(total, width), slots)


def solution(mesh):
    n = mesh.shape["seq"]
    placed = (P("seq", None, None), P("seq", None, None), P("seq", None, None), P("seq", None))
    return jax.shard_map(
        functools.partial(shards, n),
        mesh=mesh,
        in_specs=placed,
        out_specs=P("seq", None, None),
        check_vma=False,
    )
```

time: 81.2 us -> 68 us (0.84)
  Pallas kernels: 76.2 us -> 64.6 us
  local copies, waits for them, and re-layouts: 4.71 us -> 3.23 us
    pallas_call x1, Pallas kernels: 63.9 us -> 52.2 us  [shards(): pl.pallas_call(functools.partial(main_kernel, n), out_shape=jax.ShapeDtyp...]
    unnamed x1 -> x0, local copies, waits for them, and re-layouts: 1.48 us -> none
where the time goes in v2:
time: 68 us; the launch traced here: 67.8 us
  Pallas kernels  64.6 us (95%)
  local copies, waits for them, and re-layouts  3.23 us (5%)
    pallas_call x1, Pallas kernels, shards(): pl.pallas_call(functools.partial(main_kernel, n), out_shape=jax.ShapeDtyp...  52.2 us
    pallas_call x1, Pallas kernels, shards(): pl.pallas_call(functools.partial(pack_kernel, groups, capacity), out_shap...  7.04 us
    pallas_call x1, Pallas kernels, shards(): pl.pallas_call(unpack_kernel, out_shape=jax.ShapeDtypeStruct((tokens, rou...  5.36 us
    transpose x1, local copies, waits for them, and re-layouts, shards(): v8 = values.transpose(1, 0, 2)  3.23 us

profile of v2, /device:TPU:21, one launch (start us, length us, event | category | flops | bytes accessed | tf_op | source)
XLA Modules:
  0.0 67.8 jit_solution(12032181981176756883)
XLA Ops:
  0.0 7.0 %pack.1 = (bf16[2560,128]{1,0:T(8,128)(2,1)}, f32[2560,128]{1,0:T(8,128)}, s32[256,128]{1,0:T(8,128)}) custom-call(bf16[256,8,128]{2,1,0:T(8,128)(2,1)} %q_ref.1, s32[8,256]{1,0:T(8,128)} %bitcast.11), custom_call_target="tpu_custom_call" | custom-call | tf_op jit(solution)/shard_map/pack/pallas_call | solution.py:413
  7.0 3.2 %copy_bitcast_fusion = (bf16[8,512,128]{2,1,0:T(8,128)(2,1)}, bf16[8,512,128]{2,1,0:T(8,128)(2,1)}) fusion(bf16[512,8,128]{2,1,0:T(8,128)(2,1)} %param.6, bf16[512,8,128]{2,1,0:T(8,128)(2,1)} %param.5), kind=kLoop, calls=%fused_computation | loop fusion | bytes 4194304 | tf_op jit(solution)/shard_map/transpose | solution.py:426
  10.3 52.2 %main.1 = bf16[8,320,128]{2,1,0:T(8,128)(2,1)} custom-call(bf16[8,320,128]{2,1,0:T(8,128)(2,1)} %bitcast.10, f32[8,320,128]{2,1,0:T(8,128)} %bitcast.9, bf16[8,512,128]{2,1,0:T(8,128)(2,1)} %get-tuple-element.12.k8, bf16[8,512,128]{2,1,0:T(8,128)(2,1)} %get-tuple-element.11.v8), custom_call_target="tpu_custom_call" | custom-call | tf_op jit(solution)/shard_map/main/pallas_call | solution.py:431
  62.5 5.4 %unpack.1 = bf16[256,8,128]{2,1,0:T(8,128)(2,1)} custom-call(bf16[2560,128]{1,0:T(8,128)(2,1)} %bitcast.8, s32[256,128]{1,0:T(8,128)} %get-tuple-element.10.slots_ref), custom_call_target="tpu_custom_call" | custom-call | tf_op jit(solution)/shard_map/unpack/pallas_call | solution.py:458
